TPU v7x, 32 devices: a whole 2x2x4 slice. The times are simulated.
32 devices in a mesh: front: 2 (over y), row: 4 (over x, core), col: 4 (over z).
Axes of the slice: x: 2, y: 2, z: 4, core: 2. Of those that a mesh axis runs over, the one named last changes fastest.
Arguments:
- front_cols: bfloat16 [16384, 256], P(('front', 'row'), 'col'), parts along dimension 0, as said below
- contrib: bfloat16 [8, 3072, 1536], P(('front', 'col'), 'row'), parts along dimension 0, as said below
- child_blocks: int32 [4, 24], P('front'), parts along dimension 0, may hold values from 0 to 63, as said below
- child_live: int32 [4], P('front'), parts along dimension 0, may hold values from 12 to 24
- finish: int32 [8], P('front'), parts along dimension 0, may hold values from 0 to 3, as said below
Outputs:
- schur: bfloat16 [16384, 8192], P(('front', 'row'), 'col'), parts along dimension 0
There are 2 independent parts, one for each index of `front`. A program takes and returns all parts, laid end to end along the dimension named above; each array names one. Nothing has to cross between parts.
Inputs may be any that keep to these rules, and one draw needn't show every extreme that they name: `child_blocks`: row c holds distinct front blocks. With L the row sorted increasingly, entry q equals L[(q % 6) * 4 + 2 * (r % 2) + r // 2] where r = q // 6. At most 7 entries of a row lie in any aligned group of 16 consecutive block numbers, and exactly 7 in some group. `finish`: each value appears once. `contrib`: for each child c, the two pieces that finish names for c, left half then right half, form a symmetric positive definite matrix. `front_cols`: its leading 256 rows form a symmetric positive definite matrix.
All inputs are finite; a program needn't handle non-finite values.
Results may differ from a plain program's by a relative error of at most 0.008.
Values may be sent and summed in bfloat16 or wider, within the bound.
No kernel may reach another device: no remote copies, remote signals or barrier semaphores. Data moves between devices by JAX's collectives and lax.ppermute only.
A program may use at most 128 MiB of HBM per device.

v0:
```python
import jax
import jax.numpy as jnp
from jax import lax
from jax.sharding import PartitionSpec as P

PANEL = 256
BLK = 128


def from_root(x, axis, root):
    mine = lax.axis_index(axis) == root
    return lax.psum(jnp.where(mine, x, jnp.zeros_like(x)), axis)


def as_sent(x):

    def short(part):
        return part.astype(jnp.bfloat16) if part.dtype == jnp.float32 else part

    return jax.tree.map(short, x)


def one_hot(values, count):
    return values[..., None] == jnp.arange(count, dtype=jnp.int32)


def rank_within(owners):
    count = owners.shape[-1]
    places = jnp.arange(count, dtype=jnp.int32)
    same_owner = owners[..., :, None] == owners[..., None, :]
    earlier = places[None, :] < places[:, None]
    return jnp.sum(same_owner & earlier, axis=-1)


def body(front_cols, contrib, child_blocks, child_live, finish):
    row_count = lax.axis_size("row")
    col_count = lax.axis_size("col")
    own_row = lax.axis_index("row")
    own_col = lax.axis_index("col")
    local_size = front_cols.shape[0]
    group_size = local_size // BLK
    own_piece = contrib[0]
    piece_rows = own_piece.shape[0]
    piece_cols = own_piece.shape[1]
    row_blocks = piece_rows // BLK
    col_blocks = piece_cols // BLK
    spread = row_blocks + 1
    row_cap = min(row_blocks, -(-spread // row_count))
    col_cap = min(col_blocks, -(-spread // 2))
    children = child_blocks.shape[0]
    piece_child = finish // 2
    halves = finish % 2
    picked = one_hot(piece_child, children)
    column_maps = jnp.sum(jnp.where(picked[:, :, None], child_blocks[None, :, :], 0), axis=1)
    column_live = jnp.sum(jnp.where(picked, child_live[None, :], 0), axis=1)
    row_maps = column_maps.reshape(col_count, row_count, row_blocks)
    split_maps = column_maps.reshape(col_count, 2, col_blocks)
    col_maps = jnp.where(halves[:, None] == 0, split_maps[:, 0], split_maps[:, 1])
    row_owner = row_maps // group_size
    row_rank = rank_within(row_owner)
    col_owner = col_maps // group_size
    col_rank = rank_within(col_owner)
    live_rows = column_live[own_col] * BLK
    child_row = own_row * piece_rows + jnp.arange(piece_rows, dtype=jnp.int32)
    child_col = halves[own_col] * piece_cols + jnp.arange(piece_cols, dtype=jnp.int32)
    keep_mask = (
        (child_row[:, None] < live_rows)
        & (child_col[None, :] < live_rows)
        & (child_row[:, None] >= child_col[None, :])
    )
    masked = jnp.where(keep_mask, own_piece, jnp.zeros((), own_piece.dtype))
    sent_row_owner = row_owner[own_col, own_row]
    sent_row_rank = row_rank[own_col, own_row]
    sent_col_owner = col_owner[own_col]
    sent_col_rank = col_rank[own_col]
    col_select = jnp.sum(
        (col_owner == own_col)[:, :, None, None]
        & one_hot(col_rank, col_cap)[:, :, :, None]
        & one_hot(col_maps - own_col * group_size, group_size)[:, :, None, :],
        axis=1,
    ).astype(jnp.bfloat16)
    slot_total = row_cap * col_cap
    target = (
        (sent_row_owner[:, None] * col_count + sent_col_owner[None, :]) * slot_total
        + sent_row_rank[:, None] * col_cap
        + sent_col_rank[None, :]
    )
    route_table = one_hot(target, row_count * col_count * slot_total).astype(jnp.bfloat16)
    block_items = masked.reshape(row_blocks, BLK, col_blocks, BLK)
    outgoing = jnp.einsum(
        "iju,iajb->uab", route_table, block_items, preferred_element_type=jnp.float32
    )
    outgoing = outgoing.astype(jnp.bfloat16).reshape(row_count * col_count, slot_total, BLK, BLK)
    incoming = lax.all_to_all(outgoing, ("row", "col"), split_axis=0, concat_axis=0, tiled=True)
    row_select = jnp.sum(
        (row_owner == own_row)[..., None, None]
        & one_hot(row_rank, row_cap)[..., :, None]
        & one_hot(row_maps - own_row * group_size, group_size)[..., None, :],
        axis=2,
    )
    row_select = jnp.transpose(row_select, (1, 0, 2, 3)).astype(jnp.bfloat16)
    weight = row_select[:, :, :, None, :, None] * col_select[None, :, None, :, None, :]
    weight = weight.reshape(row_count * col_count, slot_total, group_size, group_size)
    assembled = jnp.einsum("xspq,xsab->paqb", weight, incoming, preferred_element_type=jnp.float32)
    assembled = assembled.reshape(local_size, local_size)
    initial = lax.all_gather(front_cols, "col", axis=1, tiled=True).astype(jnp.float32)
    initial = jnp.where(own_col == 0, initial, 0.0)
    assembled = assembled.at[:, :PANEL].add(initial)
    row_ids = own_row * local_size + jnp.arange(local_size, dtype=jnp.int32)
    col_ids = own_col * local_size + jnp.arange(local_size, dtype=jnp.int32)
    lower_part = row_ids[:, None] >= col_ids[None, :]
    assembled = jnp.where(lower_part, assembled, 0.0)
    leading = assembled[:, :PANEL]
    corner = from_root(leading[:PANEL].astype(jnp.bfloat16), "row", 0).astype(jnp.float32)
    corner = corner + jnp.tril(corner, -1).T
    corner = jnp.where(own_col == 0, corner, jnp.eye(PANEL, dtype=jnp.float32))
    factor = jnp.linalg.cholesky(corner)
    solved = lax.linalg.triangular_solve(
        factor, leading, left_side=False, lower=True, transpose_a=True
    )
    row_panel = from_root(as_sent(solved), "col", 0).astype(solved.dtype)
    col_panel = from_root(as_sent(row_panel), "row", own_col).astype(row_panel.dtype)
    update = jnp.einsum(
        "ik,jk->ij",
        row_panel,
        col_panel,
        precision=lax.Precision.HIGHEST,
        preferred_element_type=jnp.float32,
    )
    keep_out = lower_part & (row_ids[:, None] >= PANEL) & (col_ids[None, :] >= PANEL)
    return jnp.where(keep_out, assembled - update, 0.0).astype(jnp.bfloat16)


def solution(mesh):
    return jax.shard_map(
        body,
        mesh=mesh,
        in_specs=(
            P(("front", "row"), "col"),
            P(("front", "col"), "row", None),
            P("front", None),
            P("front"),
            P("front"),
        ),
        out_specs=P(("front", "row"), "col"),
        check_vma=False,
    )
```

profile of v0, /device:TPU:0, one launch (start us, length us, event | category | flops | bytes accessed | tf_op | source)
XLA Modules:
  0.0 387.8 jit_solution(2803726330560877903)
XLA Ops:
  6.5 0.7 and_select_fusion.4
  7.2 0.7 broadcast_compare_fusion.6
  7.9 0.8 select_reduce_fusion.2
  9.1 0.6 dynamic_slice.23
  9.7 0.7 select_reduce_fusion.3
  10.4 0.7 dynamic_slice.22
  12.7 0.3 convert_reduce_fusion.3
  13.3 4.2 %squeeze.13 = bf16[6,128,12,128]{3,2,1,0:T(8,128)(2,1)S(1)} reshape(bf16[1,768,1536]{2,1,0:T(8,128)(2,1)} %param.8) | data formatting | bytes 4718592 | tf_op jit(solution)/shard_map/squeeze | solution.py:42
  17.4 0.6 convert_reduce_fusion.2
  18.3 3.5 fusion.1
  21.8 3.1 copy.61
  24.9 7.4 %all-to-all-start = ((bf16[16,8,128,128]{3,1,2,0:T(8,128)(2,1)}), bf16[16,8,128,128]{3,1,2,0:T(8,128)(2,1)}, u32[]{:S(2)}, u32[]{:S(2)}) async-start(bf16[16,8,128,128]{3,1,2,0:T(8,128)(2,1)} %copy.61), calls=%async_computation | async-start | bytes 8388608 | tf_op jit(solution)/shard_map/all_to_all | solution.py:94
  32.4 0.7 all-gather.2.cloned.1.call-update
  34.2 0.6 compare_reduce_fusion.2
  34.9 76.1 %all-gather.2.cloned.1.call-done = bf16[2048,256]{0,1:T(8,128)(2,1)} async-done(((bf16[2048,64]{0,1:T(8,128)(2,1)}), bf16[2048,256]{0,1:T(8,128)(2,1)}) %all-gather.2.cloned.1.call-update) | async-done | bytes 1048592 | tf_op jit(solution)/shard_map/all_gather | solution.py:106
  111.0 1.5 copy.68
  112.5 31.0 %all-to-all-done = bf16[16,8,128,128]{3,1,2,0:T(8,128)(2,1)} async-done(((bf16[16,8,128,128]{3,1,2,0:T(8,128)(2,1)}), bf16[16,8,128,128]{3,1,2,0:T(8,128)(2,1)}, u32[]{:S(2)}, u32[]{:S(2)}) %all-to-all-start) | async-done | bytes 4194336 | tf_op jit(solution)/shard_map/all_to_all | solution.py:94
  143.5 4.9 %convolution_bitcast_fusion = f32[16,128,16,128]{3,2,0,1:T(8,128)S(1)} fusion(bf16[16,8,16]{2,1,0:T(8,128)(2,1)S(1)} %bitcast.83, bf16[16,8,16]{1,0,2:T(8,128)(2,1)S(1)} %copy.64, bf16[16,8,128,128]{3,1,2,0:T(8,128)(2,1)} %all-to-all-done), kind=kOutput, calls=%fused_computation.7 | convolution fusion | flops 1073872896 | bytes 20979712 | tf_op jit(solution)/shard_map/xspq,xsab->paqb/dot_general | solution.py:104
  148.4 6.2 %copy.67 = f32[16,128,16,128]{3,2,1,0:T(8,128)} copy(f32[16,128,16,128]{3,2,0,1:T(8,128)S(1)} %convolution_bitcast_fusion) | data formatting | bytes 33554432 | tf_op jit(solution)/shard_map/xspq,xsab->paqb/transpose | solution.py:104
  154.6 11.0 %copy.83 = f32[256,8,16,128]{3,1,2,0:T(8,128)S(1)} copy(f32[256,8,16,128]{3,2,1,0:T(8,128)} %bitcast.82) | data formatting | bytes 33554432
  165.6 1.3 fusion.7
  166.9 2.1 compare_select_fusion
  169.0 3.6 copy-done
  172.6 5.7 %copy-done.1 = f32[2048,2048]{1,0:T(8,128)} copy-done((f32[2048,2048]{1,0:T(8,128)}, f32[2048,2048]{1,0:T(8,128)S(1)}, u32[]{:S(2)}) %copy-start.1) | copy-done | bytes 16777240
  178.4 0.7 fusion.17
  179.3 30.4 %all-reduce.5.cloned.1.call-done = bf16[256,256]{1,0:T(8,128)(2,1)} async-done(((bf16[256,256]{1,0:T(8,128)(2,1)}), bf16[256,256]{1,0:T(8,128)(2,1)}) %all-reduce.5.cloned.1.call-update) | async-done | bytes 131088 | tf_op jit(solution)/shard_map/psum | solution.py:12
  209.7 1.0 copy.69
  210.8 1.0 fusion.14
  212.0 11.7 %cholesky.49 = f32[128,128]{1,0:T(8,128)S(1)} custom-call(f32[128,128]{1,0:T(8,128)S(1)} %cholesky.115), custom_call_target="Cholesky" | custom-call | tf_op jit(solution)/shard_map/jit(cholesky)/cholesky | solution.py:117
  223.7 9.8 %custom-call.14 = f32[1,128,128]{1,2,0:T(8,128)S(1)} custom-call(f32[1,128,128]{2,1,0:T(8,128)S(1)} %get-tuple-element.44), custom_call_target="InvertDiagBlocksLowerTriangular" | custom-call | tf_op jit(solution)/shard_map/jit(cholesky)/cholesky | solution.py:117
  234.0 11.7 %cholesky.103 = f32[128,128]{1,0:T(8,128)S(1)} custom-call(f32[128,128]{1,0:T(8,128)S(1)} %convolution_subtract_fusion.1), custom_call_target="Cholesky" | custom-call | tf_op jit(solution)/shard_map/jit(cholesky)/cholesky | solution.py:117
  245.8 0.7 compare_reduce_fusion
  246.5 0.6 compare_reduce_fusion.1
  248.6 4.2 %while.2 = (s32[]{:T(128)}, f32[256,256]{1,0:T(8,128)S(1)}, s32[2,2]{1,0:T(2,128)S(1)}, f32[2,128,128]{2,1,0:T(8,128)S(1)}, s32[]{:T(128)}) while((s32[]{:T(128)}, f32[256,256]{1,0:T(8,128)S(1)}, s32[2,2]{1,0:T(2,128)S(1)}, f32[2,128,128]{2,1,0:T(8,128)S(1)}, s32[]{:T(128)}) %tuple.33), condition=%wide.while_cond.1, body=%wide.while_body.1.sunk | while | flops 2 | bytes 131181 | solution.py:118
  248.8 0.6 fusion.42
  249.3 1.4 bitcast_dynamic-update-slice_fusion.2
  250.8 0.6 fusion.42
  251.4 1.4 bitcast_dynamic-update-slice_fusion.2
  252.8 19.7 %custom-call.15 = f32[2,128,128]{1,2,0:T(8,128)S(1)} custom-call(f32[2,128,128]{2,1,0:T(8,128)S(1)} %get-tuple-element.24), custom_call_target="InvertDiagBlocksLowerTriangular" | custom-call | tf_op jit(solution)/shard_map/triangular_solve | solution.py:118
  272.5 2.3 fusion.9
  274.8 3.0 convolution_subtract_fusion
  277.8 0.3 copy.71
  278.1 1.0 convolution_convert_fusion
  279.1 1.2 maximum_select_fusion
  280.3 52.0 %all-reduce.7.cloned.1.call-done = bf16[2048,256]{1,0:T(8,128)(2,1)} async-done(((bf16[2048,256]{1,0:T(8,128)(2,1)}), bf16[2048,256]{1,0:T(8,128)(2,1)}) %all-reduce.7.cloned.1.call-update) | async-done | bytes 1048592 | tf_op jit(solution)/shard_map/psum | solution.py:12
  332.3 2.3 broadcast_select_fusion
  334.6 35.7 %all-reduce.9.cloned.1.call-done = bf16[2048,256]{1,0:T(8,128)(2,1)} async-done(((bf16[2048,256]{1,0:T(8,128)(2,1)}), bf16[2048,256]{1,0:T(8,128)(2,1)}) %all-reduce.9.cloned.1.call-update) | async-done | bytes 1048592 | tf_op jit(solution)/shard_map/psum | solution.py:12
  370.3 11.0 %select_convert_fusion = bf16[2048,2048]{1,0:T(8,128)(2,1)} fusion(bf16[2048,256]{1,0:T(8,128)(2,1)} %all-reduce.7.cloned.1.call-done, bf16[2048,256]{1,0:T(8,128)(2,1)} %all-reduce.9.cloned.1.call-done, s32[2048]{0:T(1024)S(1)} %get-tuple-element.52, s32[2048]{0:T(1024)S(1)} %get-tuple-element.53, pred[2048]{0:T(1024)(128)(4,1)S(1)} %broadcast_compare_fusion.3, ...), kind=kOutput, calls=%fused_computation.5 | convolution fusion | flops 2176843776 | bytes 27283456 | tf_op jit(solution)/shard_map/ik,jk->ij/dot_general | solution.py:123
  (62 shorter events, 3.5 us)
Async XLA Ops:
  24.9 118.6 %all-to-all-start = ((bf16[16,8,128,128]{3,1,2,0:T(8,128)(2,1)}), bf16[16,8,128,128]{3,1,2,0:T(8,128)(2,1)}, u32[]{:S(2)}, u32[]{:S(2)}) async-start(bf16[16,8,128,128]{3,1,2,0:T(8,128)(2,1)} %copy.61), calls=%async_computation | async-start | bytes 8388608 | tf_op jit(solution)/shard_map/all_to_all | solution.py:94
  32.4 78.6 %all-gather.2.cloned.1.call-start = ((), (), s32[]{:S(2)}) async-start(), calls=%async_computation.1 | async-start | bytes 1310720 | tf_op jit(solution)/shard_map/all_gather | solution.py:106
  33.1 176.6 %all-reduce.5.cloned.1.call-start = ((), (), s32[]{:S(2)}) async-start(), calls=%async_computation.2 | async-start | bytes 262144 | tf_op jit(solution)/shard_map/psum | solution.py:12
  166.9 5.7 %copy-start = (f32[2048,2048]{1,0:T(8,128)}, f32[2048,2048]{1,0:T(8,128)S(1)}, u32[]{:S(2)}) copy-start(f32[2048,2048]{1,0:T(8,128)S(1)} %fusion.7) | copy-start | bytes 50331652
  172.6 5.7 %copy-start.1 = (f32[2048,2048]{1,0:T(8,128)}, f32[2048,2048]{1,0:T(8,128)S(1)}, u32[]{:S(2)}) copy-start(f32[2048,2048]{1,0:T(8,128)S(1)} %compare_select_fusion) | copy-start | bytes 50331652
  179.1 153.3 %all-reduce.7.cloned.1.call-start = ((), (), s32[]{:S(2)}) async-start(), calls=%async_computation.3 | async-start | bytes 2097152 | tf_op jit(solution)/shard_map/psum | solution.py:12
  280.3 90.0 %all-reduce.9.cloned.1.call-start = ((), (), s32[]{:S(2)}) async-start(), calls=%async_computation.4 | async-start | bytes 2097152 | tf_op jit(solution)/shard_map/psum | solution.py:12
Sparse Core Ops, SparseCore 0:
  34.8 76.1 all-gather.1
  179.2 30.5 all-reduce.4
  280.4 51.8 all-reduce.6
  334.7 35.5 all-reduce.8
where the time goes:
time: 388 us
  waiting for transfers between devices  226 us (58%)
  other arithmetic  68.4 us (18%)
  local copies, waits for them, and re-layouts  43.1 us (11%)
  matrix products  26.2 us (7%)
  between operations  16.1 us (4%)
  starting transfers between devices  7.78 us (2%)
    psum x3, waiting for transfers between devices, from_root(): return lax.psum(jnp.where(mine, x, jnp.zeros_like(x)), axis)  118 us
    all_gather x1, waiting for transfers between devices, body(): lax.all_gather(front_cols, 'col', axis=1, tiled=True).astype(jnp.float32)  76.1 us
    another operation x7, other arithmetic, body(): factor = jnp.linalg.cholesky(corner)  34.6 us
    all_to_all x1, waiting for transfers between devices, body(): lax.all_to_all(outgoing, ('row', 'col'), split_axis=0, concat_axis=0, til...  31 us
    unnamed x5, local copies, waits for them, and re-layouts  20.3 us
    another operation x3, other arithmetic, body(): lax.linalg.triangular_solve(factor, leading, left_side=False, lower=True,...  19.7 us
    dot_general x1, matrix products, body(): jnp.einsum('ik,jk->ij', row_panel, col_panel, precision=lax.Precision.HIG...  11 us
  transfers between devices with their start and end apart: 5, of which 5 were waited for; matrix products, arithmetic and copies ran while one was open for 1% of the time, Pallas kernels for 0%

commit v1 on v0

--- a/solution.py
+++ b/solution.py
@@ -9,7 +9,7 @@
 
 def from_root(x, axis, root):
     mine = lax.axis_index(axis) == root
-    return lax.psum(jnp.where(mine, x, jnp.zeros_like(x)), axis)
+    return jnp.sum(lax.all_gather(jnp.where(mine, x, jnp.zeros_like(x)), axis), axis=0)
 
 
 def as_sent(x):

time: 388 us -> 415 us (1.070); the launches traced: 388 us -> 407 us
  local copies, waits for them, and re-layouts: 43.1 us -> 51.6 us
  other arithmetic: 68.4 us -> 75.6 us
  blocking collectives: 0 us -> 7.17 us
  waiting for transfers between devices: 226 us -> 221 us
    psum x3 -> x0, waiting for transfers between devices: 118 us -> none  [from_root(): return lax.psum(jnp.where(mine, x, jnp.zeros_like(x)), axis)]
    all_gather x0 -> x2, waiting for transfers between devices: none -> 113 us  [from_root(): lax.all_gather(jnp.where(mine, x, jnp.zeros_like(x)), axis)]
    all_gather x0 -> x1, local copies, waits for them, and re-layouts: none -> 7.81 us  [from_root(): lax.all_gather(jnp.where(mine, x, jnp.zeros_like(x)), axis)]
    reduce_sum x0 -> x2, other arithmetic: none -> 7.42 us  [from_root(): jnp.sum(lax.all_gather(jnp.where(mine, x, jnp.zeros_like(x)), axis), axis=0)]
    all_gather x0 -> x1, blocking collectives: none -> 7.17 us  [from_root(): lax.all_gather(jnp.where(mine, x, jnp.zeros_like(x)), axis)]
    unnamed x5 -> x6, local copies, waits for them, and re-layouts: 20.3 us -> 21.2 us
    another operation x3 -> x4, other arithmetic: 19.7 us -> 19.8 us  [body(): lax.linalg.triangular_solve(factor, leading, left_side=False, lower=True,...]
  transfers between devices with their start and end apart: 5 -> 4, of which waited for: 5 -> 4; matrix products, arithmetic and copies ran while one was open for 1% -> 1% of each run, Pallas kernels for 0% -> 0%
where the time goes in v1:
time: 415 us; the launch traced here: 407 us
  waiting for transfers between devices  221 us (53%)
  other arithmetic  75.6 us (18%)
  local copies, waits for them, and re-layouts  51.6 us (12%)
  matrix products  28 us (7%)
  between operations  16.3 us (4%)
  starting transfers between devices  7.56 us (2%)
  blocking collectives  7.17 us (2%)
    all_gather x2, waiting for transfers between devices, from_root(): lax.all_gather(jnp.where(mine, x, jnp.zeros_like(x)), axis)  113 us
    all_gather x1, waiting for transfers between devices, body(): lax.all_gather(front_cols, 'col', axis=1, tiled=True).astype(jnp.float32)  76.1 us
    another operation x7, other arithmetic, body(): factor = jnp.linalg.cholesky(corner)  34.6 us
    all_to_all x1, waiting for transfers between devices, body(): lax.all_to_all(outgoing, ('row', 'col'), split_axis=0, concat_axis=0, til...  31 us
    unnamed x6, local copies, waits for them, and re-layouts  21.2 us
    another operation x4, other arithmetic, body(): lax.linalg.triangular_solve(factor, leading, left_side=False, lower=True,...  19.8 us
    dot_general x1, matrix products, body(): jnp.einsum('ik,jk->ij', row_panel, col_panel, precision=lax.Precision.HIG...  12.6 us
  transfers between devices with their start and end apart: 4, of which 4 were waited for; matrix products, arithmetic and copies ran while one was open for 1% of the time, Pallas kernels for 0%

profile of v1, /device:TPU:0, one launch (start us, length us, event | category | flops | bytes accessed | tf_op | source)
XLA Modules:
  0.0 407.2 jit_solution(5608182959456427355)
XLA Ops:
  6.5 0.7 and_select_fusion.4
  7.2 0.7 broadcast_compare_fusion.6
  7.9 0.8 select_reduce_fusion.2
  9.1 0.6 dynamic_slice.23
  9.7 0.7 select_reduce_fusion.3
  10.4 0.7 dynamic_slice.22
  12.7 0.3 convert_reduce_fusion.3
  13.3 4.2 %squeeze.13 = bf16[6,128,12,128]{3,2,1,0:T(8,128)(2,1)S(1)} reshape(bf16[1,768,1536]{2,1,0:T(8,128)(2,1)} %param.8) | data formatting | bytes 4718592 | tf_op jit(solution)/shard_map/squeeze | solution.py:42
  17.4 0.6 convert_reduce_fusion.2
  18.3 3.5 fusion.1
  21.8 3.1 copy.66
  24.9 7.4 %all-to-all-start = ((bf16[16,8,128,128]{3,1,2,0:T(8,128)(2,1)}), bf16[16,8,128,128]{3,1,2,0:T(8,128)(2,1)}, u32[]{:S(2)}, u32[]{:S(2)}) async-start(bf16[16,8,128,128]{3,1,2,0:T(8,128)(2,1)} %copy.66), calls=%async_computation | async-start | bytes 8388608 | tf_op jit(solution)/shard_map/all_to_all | solution.py:94
  32.4 0.7 all-gather.6.cloned.1.call-update
  34.2 0.6 compare_reduce_fusion.2
  34.9 76.1 %all-gather.6.cloned.1.call-done = bf16[2048,256]{0,1:T(8,128)(2,1)} async-done(((bf16[2048,64]{0,1:T(8,128)(2,1)}), bf16[2048,256]{0,1:T(8,128)(2,1)}) %all-gather.6.cloned.1.call-update) | async-done | bytes 1048592 | tf_op jit(solution)/shard_map/all_gather | solution.py:106
  111.0 1.5 copy.73
  112.5 31.0 %all-to-all-done = bf16[16,8,128,128]{3,1,2,0:T(8,128)(2,1)} async-done(((bf16[16,8,128,128]{3,1,2,0:T(8,128)(2,1)}), bf16[16,8,128,128]{3,1,2,0:T(8,128)(2,1)}, u32[]{:S(2)}, u32[]{:S(2)}) %all-to-all-start) | async-done | bytes 4194336 | tf_op jit(solution)/shard_map/all_to_all | solution.py:94
  143.5 4.9 %convolution_bitcast_fusion = f32[16,128,16,128]{3,2,0,1:T(8,128)S(1)} fusion(bf16[16,8,16]{2,1,0:T(8,128)(2,1)S(1)} %bitcast.85, bf16[16,8,16]{1,0,2:T(8,128)(2,1)S(1)} %copy.69, bf16[16,8,128,128]{3,1,2,0:T(8,128)(2,1)} %all-to-all-done), kind=kOutput, calls=%fused_computation.7 | convolution fusion | flops 1073872896 | bytes 20979712 | tf_op jit(solution)/shard_map/xspq,xsab->paqb/dot_general | solution.py:104
  148.4 6.2 %copy.72 = f32[16,128,16,128]{3,2,1,0:T(8,128)} copy(f32[16,128,16,128]{3,2,0,1:T(8,128)S(1)} %convolution_bitcast_fusion) | data formatting | bytes 33554432 | tf_op jit(solution)/shard_map/xspq,xsab->paqb/transpose | solution.py:104
  154.6 11.0 %copy.88 = f32[256,8,16,128]{3,1,2,0:T(8,128)S(1)} copy(f32[256,8,16,128]{3,2,1,0:T(8,128)} %bitcast.83) | data formatting | bytes 33554432
  165.6 1.3 fusion.8
  166.9 2.1 compare_select_fusion
  169.0 3.6 copy-done
  172.7 5.7 %copy-done.1 = f32[2048,2048]{1,0:T(8,128)} copy-done((f32[2048,2048]{1,0:T(8,128)}, f32[2048,2048]{1,0:T(8,128)S(1)}, u32[]{:S(2)}) %copy-start.1) | copy-done | bytes 16777240
  178.4 7.2 %all-gather = bf16[1024,256]{1,0:T(8,128)(2,1)S(1)} all-gather(bf16[256,256]{1,0:T(8,128)(2,1)S(1)} %fusion.21), channel_id=2, replica_groups=mesh['front'=2,'row'=4,'col'=4] {'row'}, dimensions={0}, use_global_device_ids=true | all-gather | bytes 655360 | tf_op jit(solution)/shard_map/all_gather | solution.py:12
  185.9 11.7 %cholesky.49 = f32[128,128]{1,0:T(8,128)S(1)} custom-call(f32[128,128]{1,0:T(8,128)S(1)} %cholesky.115), custom_call_target="Cholesky" | custom-call | tf_op jit(solution)/shard_map/jit(cholesky)/cholesky | solution.py:117
  197.7 9.8 %custom-call.14 = f32[1,128,128]{1,2,0:T(8,128)S(1)} custom-call(f32[1,128,128]{2,1,0:T(8,128)S(1)} %get-tuple-element.44), custom_call_target="InvertDiagBlocksLowerTriangular" | custom-call | tf_op jit(solution)/shard_map/jit(cholesky)/cholesky | solution.py:117
  208.0 11.7 %cholesky.103 = f32[128,128]{1,0:T(8,128)S(1)} custom-call(f32[128,128]{1,0:T(8,128)S(1)} %convolution_subtract_fusion.1), custom_call_target="Cholesky" | custom-call | tf_op jit(solution)/shard_map/jit(cholesky)/cholesky | solution.py:117
  219.8 0.7 compare_reduce_fusion
  220.4 0.6 compare_reduce_fusion.1
  222.4 4.1 while.2
  222.6 0.6 fusion.46
  223.2 1.3 bitcast_dynamic-update-slice_fusion.2
  224.6 0.6 fusion.46
  225.2 1.3 bitcast_dynamic-update-slice_fusion.2
  226.5 19.7 %custom-call.15 = f32[2,128,128]{1,2,0:T(8,128)S(1)} custom-call(f32[2,128,128]{2,1,0:T(8,128)S(1)} %get-tuple-element.24), custom_call_target="InvertDiagBlocksLowerTriangular" | custom-call | tf_op jit(solution)/shard_map/triangular_solve | solution.py:118
  246.2 2.3 fusion.10
  248.5 3.0 convolution_subtract_fusion
  251.6 1.1 fusion.7
  252.9 1.3 copy.76
  254.3 79.9 %all-gather.8.cloned.1.call-done = bf16[4,2048,256]{2,1,0:T(8,128)(2,1)} async-done(((bf16[1,2048,256]{2,1,0:T(8,128)(2,1)}), bf16[4,2048,256]{2,1,0:T(8,128)(2,1)}) %all-gather.8.cloned.1.call-update) | async-done | bytes 4194320 | tf_op jit(solution)/shard_map/all_gather | solution.py:12
  334.2 3.5 reduce_sum.97
  337.6 0.9 copy.83
  338.5 1.0 broadcast_select_fusion
  339.6 33.1 %all-gather.10.cloned.1.call-done = bf16[8192,256]{0,1:T(8,128)(2,1)} async-done(((bf16[2048,256]{0,1:T(8,128)(2,1)}), bf16[8192,256]{0,1:T(8,128)(2,1)}) %all-gather.10.cloned.1.call-update) | async-done | bytes 4194320 | tf_op jit(solution)/shard_map/all_gather | solution.py:12
  372.7 7.8 %reshape.524 = bf16[4,2048,256]{1,0,2:T(4,128)(2,1)} reshape(bf16[8192,256]{0,1:T(8,128)(2,1)} %all-gather.10.cloned.1.call-done) | data formatting | bytes 8388608 | tf_op jit(solution)/shard_map/all_gather | solution.py:12
  380.5 7.3 %reduce_sum.98 = bf16[2048,256]{0,1:T(8,128)(2,1)S(1)} reduce(bf16[4,2048,256]{1,0,2:T(4,128)(2,1)} %reshape.524, bf16[]{:T(256)} %constant.188.clone.1), dimensions={0}, to_apply=%region_13.14 | reduce | flops 1572864 | bytes 5242882 | tf_op jit(solution)/shard_map/reduce_sum | solution.py:12
  387.8 12.6 %select_convert_fusion = bf16[2048,2048]{1,0:T(8,128)(2,1)} fusion(bf16[2048,256]{1,0:T(8,128)(2,1)S(1)} %reduce_sum.97, bf16[2048,256]{0,1:T(8,128)(2,1)S(1)} %reduce_sum.98, s32[2048]{0:T(1024)S(1)} %get-tuple-element.52, s32[2048]{0:T(1024)S(1)} %get-tuple-element.53, pred[2048]{0:T(1024)(128)(4,1)S(1)} %broadcast_compare_fusion.3, ...), kind=kOutput, calls=%fused_computation.5 | convolution fusion | flops 2176843776 | bytes 27283456 | tf_op jit(solution)/shard_map/ik,jk->ij/dot_general | solution.py:123
  (65 shorter events, 3.7 us)
Async XLA Ops:
  24.9 118.6 %all-to-all-start = ((bf16[16,8,128,128]{3,1,2,0:T(8,128)(2,1)}), bf16[16,8,128,128]{3,1,2,0:T(8,128)(2,1)}, u32[]{:S(2)}, u32[]{:S(2)}) async-start(bf16[16,8,128,128]{3,1,2,0:T(8,128)(2,1)} %copy.66), calls=%async_computation | async-start | bytes 8388608 | tf_op jit(solution)/shard_map/all_to_all | solution.py:94
  32.4 78.6 %all-gather.6.cloned.1.call-start = ((), (), s32[]{:S(2)}) async-start(), calls=%async_computation.1 | async-start | bytes 1310720 | tf_op jit(solution)/shard_map/all_gather | solution.py:106
  33.1 301.1 %all-gather.8.cloned.1.call-start = ((), (), s32[]{:S(2)}) async-start(), calls=%async_computation.2 | async-start | bytes 5242880 | tf_op jit(solution)/shard_map/all_gather | solution.py:12
  166.9 5.7 %copy-start = (f32[2048,2048]{1,0:T(8,128)}, f32[2048,2048]{1,0:T(8,128)S(1)}, u32[]{:S(2)}) copy-start(f32[2048,2048]{1,0:T(8,128)S(1)} %fusion.8) | copy-start | bytes 50331652
  172.6 5.7 %copy-start.1 = (f32[2048,2048]{1,0:T(8,128)}, f32[2048,2048]{1,0:T(8,128)S(1)}, u32[]{:S(2)}) copy-start(f32[2048,2048]{1,0:T(8,128)S(1)} %compare_select_fusion) | copy-start | bytes 50331652
  254.3 118.4 %all-gather.10.cloned.1.call-start = ((), (), s32[]{:S(2)}) async-start(), calls=%async_computation.3 | async-start | bytes 5242880 | tf_op jit(solution)/shard_map/all_gather | solution.py:12
Sparse Core Ops, SparseCore 0:
  34.8 76.1 all-gather.5
  254.4 79.7 all-gather.7
  339.7 32.9 all-gather.9
